TPU v7x, 32 devices: a 4x2x2 block of a 4x4x8 slice. The times are simulated.
32 devices in a mesh: dp: 4 (over y, z), ep: 8 (over x, core).
Axes of the slice: x: 4, y: 2, z: 2, core: 2. Of those that a mesh axis runs over, the one named last changes fastest.
The devices are a block of a 4x4x8 slice.
Arguments:
- tokens: bfloat16 [4096, 2048], P(('dp', 'ep')), parts along dimension 0
- expert_ids: int32 [4096, 8], P(('dp', 'ep')), parts along dimension 0
- norm_gain: bfloat16 [2048], replicated
- w_router: bfloat16 [2048, 64], replicated
- w_gate: bfloat16 [64, 2048, 1024], P('ep')
- w_up: bfloat16 [64, 2048, 1024], P('ep')
- w_down: bfloat16 [64, 1024, 2048], P('ep')
Outputs:
- output: bfloat16 [4096, 2048], P(('dp', 'ep')), parts along dimension 0
There are 4 independent parts. A program takes and returns all parts, laid end to end along the dimension named above; an argument that names none is the same for every part.
All inputs are finite; a program needn't handle non-finite values.
Results may differ from a plain program's by a relative error of at most 0.00573975.
Values are sent between devices in bfloat16 or wider.
A program may use at most 768 MiB of HBM per device.

v0:
```python
import jax
import jax.numpy as jnp
from jax import lax
from jax.sharding import PartitionSpec as P

NORM_EPS = 1e-5


def rms_norm(tok_rows, norm_gain):
    tok32 = tok_rows.astype(jnp.float32)
    inv_rms = lax.rsqrt(jnp.mean(tok32 * tok32, axis=1, keepdims=True) + NORM_EPS)
    return (tok32 * inv_rms * norm_gain.astype(jnp.float32)).astype(jnp.bfloat16)


def expert_ffn(rows, w_gate, w_up, w_down, group_sizes):
    hidden_gate = lax.ragged_dot(rows, w_gate, group_sizes, preferred_element_type=jnp.float32)
    hidden_up = lax.ragged_dot(rows, w_up, group_sizes, preferred_element_type=jnp.float32)
    swiglu_out = (jax.nn.silu(hidden_gate) * hidden_up).astype(jnp.bfloat16)
    return lax.ragged_dot(swiglu_out, w_down, group_sizes, preferred_element_type=jnp.float32).astype(jnp.bfloat16)


def route_plan(expert_ids, ep_size, e_local, send_max):
    tok_count, top_k = expert_ids.shape
    pairs = tok_count * top_k
    flat_ids = expert_ids.reshape(pairs)
    sort_order = jnp.argsort(flat_ids, stable=True)
    sorted_dev = flat_ids[sort_order] // e_local
    expert_count = jnp.bincount(flat_ids, length=ep_size * e_local).astype(jnp.int32)
    dev_count = expert_count.reshape(ep_size, e_local).sum(axis=1)
    dev_start = jnp.cumsum(dev_count) - dev_count
    slot_sorted = sorted_dev * send_max + jnp.arange(pairs) - dev_start[sorted_dev]
    slot_of_pair = jnp.zeros((pairs,), jnp.int32).at[sort_order].set(slot_sorted)
    sorted_pos = jnp.minimum(dev_start[:, None] + jnp.arange(send_max)[None, :], pairs - 1)
    send_tok = (sort_order[sorted_pos] // top_k).reshape(ep_size * send_max)
    return expert_count.reshape(ep_size, e_local), slot_of_pair, send_tok


def recv_plan(recv_count, send_max, recv_max):
    ep_size, e_local = recv_count.shape
    row_end = jnp.cumsum(recv_count, axis=1)
    row_begin = row_end - recv_count
    slot_rank = jnp.arange(send_max)
    slot_expert = jnp.sum(row_end[:, None, :] <= slot_rank[None, :, None], axis=2)
    expert_safe = jnp.minimum(slot_expert, e_local - 1)
    expert_total = recv_count.sum(axis=0)
    expert_start = jnp.cumsum(expert_total) - expert_total
    src_before = jnp.cumsum(recv_count, axis=0) - recv_count
    offset = expert_start[None, :] + src_before - row_begin
    compact_pos = jnp.where(slot_expert < e_local, jnp.take_along_axis(offset, expert_safe, axis=1) + slot_rank[None, :], recv_max).reshape(ep_size * send_max)
    compact_src = jnp.zeros((recv_max,), jnp.int32).at[compact_pos].set(jnp.arange(ep_size * send_max), mode='drop')
    return expert_total, compact_src, jnp.minimum(compact_pos, recv_max - 1)


def solution(mesh):
    ep_size = mesh.shape['ep']

    def device_step(tokens, expert_ids, norm_gain, w_router, w_gate, w_up, w_down):
        tok_count, top_k = expert_ids.shape
        width = tokens.shape[1]
        e_local = w_gate.shape[0]
        pairs = tok_count * top_k
        send_max = 2 * pairs // ep_size
        recv_max = 3 * pairs // 2
        normed = rms_norm(tokens, norm_gain)
        router_prob = jax.nn.softmax(jnp.dot(normed, w_router, preferred_element_type=jnp.float32), axis=1)
        gate_vals = jnp.take_along_axis(router_prob, expert_ids, axis=1)
        send_count, slot_of_pair, send_tok = route_plan(expert_ids, ep_size, e_local, send_max)
        send_rows = normed[send_tok].reshape(ep_size, send_max, width)
        recv_count = lax.all_to_all(send_count, 'ep', 0, 0, tiled=True)
        recv_rows = lax.all_to_all(send_rows, 'ep', 0, 0, tiled=True)
        expert_total, compact_src, back_pos = recv_plan(recv_count, send_max, recv_max)
        compact_rows = recv_rows.reshape(ep_size * send_max, width)[compact_src]
        expert_out = expert_ffn(compact_rows, w_gate, w_up, w_down, expert_total)
        back_rows = expert_out[back_pos].reshape(ep_size, send_max, width)
        home_rows = lax.all_to_all(back_rows, 'ep', 0, 0, tiled=True)
        pair_out = home_rows.reshape(ep_size * send_max, width)[slot_of_pair].reshape(tok_count, top_k, width)
        moe_sum = jnp.sum(gate_vals[:, :, None] * pair_out, axis=1)
        return (tokens.astype(jnp.float32) + moe_sum).astype(jnp.bfloat16)

    row_spec = P(('dp', 'ep'), None)
    expert_spec = P('ep', None, None)
    return jax.shard_map(device_step, mesh=mesh, in_specs=(row_spec, row_spec, P(None), P(None, None), expert_spec, expert_spec, expert_spec), out_specs=row_spec, check_vma=False)
```

profile of v0, /device:TPU:81, one launch (start us, length us, event | category | flops | bytes accessed | tf_op | source)
XLA Modules:
  0.0 398.1 jit_solution(6272665862101883875)
XLA Ops:
  0.0 0.8 broadcast_maximum_fusion
  0.8 0.1 copy.35
  0.9 0.1 reshape.509
  1.0 7.6 %scatter_custom_fusion = s32[64]{0:T(128)S(1)} fusion(s32[1024]{0:T(1024)S(1)} %reshape.509, s32[1024]{0:T(1024)S(1)} %broadcast.445, s32[]{:T(128)} %constant.46.clone.1), kind=kCustom, calls=%fused_computation.90 | custom fusion | flops 1024 | bytes 260 | tf_op jit(solution)/shard_map/scatter-add | solution.py:28
  8.6 0.7 all_to_all.15
  9.3 6.0 %all-to-all-start.1 = ((s32[8,1,8]{2,1,0:T(1,128)}), s32[8,1,8]{2,1,0:T(1,128)S(1)}, u32[]{:S(2)}, u32[]{:S(2)}) async-start(s32[8,1,8]{2,1,0:T(1,128)} %bitcast.1), calls=%async_computation.1 | async-start | bytes 8192 | tf_op jit(solution)/shard_map/all_to_all | solution.py:69
  15.4 0.8 copy.37
  16.1 1.2 fusion.1
  17.4 0.7 convert_element_type.29
  18.1 0.1 reduce_sum.56
  18.2 0.2 reduce-window.15
  18.5 0.1 reshape.421
  18.6 4.4 %sort.17 = (s32[1024]{0:T(1024)}, s32[1024]{0:T(1024)S(1)}) sort(s32[1024]{0:T(1024)S(1)} %reshape.421, s32[1024]{0:T(1024)S(1)} %iota.21), dimensions={0}, to_apply=%region_3.0 | sort | flops 10240 | bytes 16384 | tf_op jit(solution)/shard_map/jit(argsort)/sort | solution.py:26
  23.0 8.6 %gather_fusion = s32[2048]{0:T(1024)S(1)} fusion(s32[1024]{0:T(1024)S(1)} %get-tuple-element.6, s32[2048]{0:T(1024)S(1)} %broadcast_clamp_fusion.2), kind=kCustom, calls=%fused_computation | custom fusion | bytes 24576 | tf_op jit(solution)/shard_map/gather | solution.py:34
  31.6 0.2 fusion.3
  31.8 11.0 %gather_fusion.1 = bf16[2048,2048]{1,0:T(8,128)(2,1)} fusion(bf16[128,2048]{1,0:T(8,128)(2,1)S(1)} %fusion.3, s32[2048]{0:T(1024)S(1)} %broadcast_clamp_fusion.1), kind=kCustom, calls=%fused_computation.1 | custom fusion | bytes 16785408 | tf_op jit(solution)/shard_map/gather | solution.py:68
  42.9 5.1 %all-to-all-start = ((bf16[8,256,2048]{2,1,0:T(8,128)(2,1)}), bf16[8,256,2048]{2,1,0:T(8,128)(2,1)}, u32[]{:S(2)}, u32[]{:S(2)}) async-start(bf16[8,256,2048]{2,1,0:T(8,128)(2,1)} %bitcast.65), calls=%async_computation | async-start | bytes 16777216 | tf_op jit(solution)/shard_map/all_to_all | solution.py:70
  48.0 0.2 reduce_window_sum.31
  48.1 0.5 reduce_sum.58
  48.7 1.5 ragged-dot-metadata
  50.2 0.8 reduce-window.16
  51.0 0.1 convert_reduce_fusion
  51.2 0.7 bitcast_subtract_fusion
  51.9 9.1 %gather_fusion.7 = s32[2048]{0:T(1024)S(1)} fusion(s32[8,8]{1,0:T(8,128)S(1)} %subtract_subtract_fusion, s32[2048]{0:T(1024)S(1)} %bitcast.63), kind=kCustom, calls=%fused_computation.7 | custom fusion | bytes 32768 | tf_op jit(solution)/shard_map/jit(take_along_axis)/gather | solution.py:49
  61.1 8.0 %scatter_custom_fusion.1 = s32[1536]{0:T(1024)S(1)} fusion(s32[2048]{0:T(1024)S(1)} %bitcast.79, s32[2048]{0:T(1024)S(1)} %iota.22, s32[]{:T(128)} %constant.46.clone.1), kind=kCustom, calls=%fused_computation.79 | custom fusion | bytes 6148 | tf_op jit(solution)/shard_map/scatter | solution.py:50
  69.2 72.1 %all-to-all-done = bf16[8,256,2048]{2,1,0:T(8,128)(2,1)} async-done(((bf16[8,256,2048]{2,1,0:T(8,128)(2,1)}), bf16[8,256,2048]{2,1,0:T(8,128)(2,1)}, u32[]{:S(2)}, u32[]{:S(2)}) %all-to-all-start) | async-done | bytes 8388640 | tf_op jit(solution)/shard_map/all_to_all | solution.py:70
  141.3 17.1 %gather_fusion.2 = bf16[1536,2048]{1,0:T(8,128)(2,1)} fusion(bf16[2048,2048]{1,0:T(8,128)(2,1)} %bitcast.7, s32[2048]{0:T(1024)S(1)} %pad_clamp_fusion), kind=kCustom, calls=%fused_computation.2 | custom fusion | bytes 12589056 | tf_op jit(solution)/shard_map/gather | solution.py:72
  158.5 24.7 %ragged-dot-none.2 = f32[1536,1024]{1,0:T(8,128)} custom-call(s32[1]{0:T(128)} %get-tuple-element.7, s32[9]{0:T(128)} %get-tuple-element.8, s32[13]{0:T(128)} %get-tuple-element.9, s32[13]{0:T(128)} %get-tuple-element.10, s32[1]{0:T(128)} %get-tuple-element.7, bf16[1536,2048]{1,0:T(8,128)(2,1)} %gather_fusion.2, bf16[8,2048,1024]{2,1,0:T(8,128)(2,1)} %param.11), custom_call_target="tpu_custom_call" | custom-call | flops 6442450944 | bytes 46137376 | tf_op jit(solution)/shard_map/ragged_dot_general/ragged-dot-none
  183.2 24.7 %ragged-dot-none.1 = f32[1536,1024]{1,0:T(8,128)} custom-call(s32[1]{0:T(128)} %get-tuple-element.7, s32[9]{0:T(128)} %get-tuple-element.8, s32[13]{0:T(128)} %get-tuple-element.9, s32[13]{0:T(128)} %get-tuple-element.10, s32[1]{0:T(128)} %get-tuple-element.7, bf16[1536,2048]{1,0:T(8,128)(2,1)} %gather_fusion.2, bf16[8,2048,1024]{2,1,0:T(8,128)(2,1)} %param.12), custom_call_target="tpu_custom_call" | custom-call | flops 6442450944 | bytes 46137376 | tf_op jit(solution)/shard_map/ragged_dot_general/ragged-dot-none
  207.9 6.8 %multiply_convert_fusion = bf16[1536,1024]{1,0:T(8,128)(2,1)} fusion(f32[1536,1024]{1,0:T(8,128)} %ragged-dot-none.1, f32[1536,1024]{1,0:T(8,128)} %ragged-dot-none.2), kind=kLoop, calls=%fused_computation.13 | loop fusion | flops 9437184 | bytes 15728640 | tf_op jit(solution)/shard_map/convert_element_type | solution.py:18
  214.7 26.1 %ragged-dot-none = f32[1536,2048]{1,0:T(8,128)} custom-call(s32[1]{0:T(128)} %get-tuple-element.7, s32[9]{0:T(128)} %get-tuple-element.8, s32[13]{0:T(128)} %get-tuple-element.9, s32[13]{0:T(128)} %get-tuple-element.10, s32[1]{0:T(128)} %get-tuple-element.7, bf16[1536,1024]{1,0:T(8,128)(2,1)} %multiply_convert_fusion, bf16[8,1024,2048]{2,1,0:T(8,128)(2,1)} %param.13), custom_call_target="tpu_custom_call" | custom-call | flops 6442450944 | bytes 49283104 | tf_op jit(solution)/shard_map/ragged_dot_general/ragged-dot-none
  240.8 8.2 %convert_element_type.33 = bf16[1536,2048]{1,0:T(8,128)(2,1)} convert(f32[1536,2048]{1,0:T(8,128)} %ragged-dot-none) | non-fusion elementwise | flops 3145728 | bytes 18874368 | tf_op jit(solution)/shard_map/convert_element_type | solution.py:19
  249.0 19.9 %gather_fusion.3 = bf16[2048,2048]{1,0:T(8,128)(2,1)} fusion(bf16[1536,2048]{1,0:T(8,128)(2,1)} %convert_element_type.33, s32[2048]{0:T(1024)S(1)} %broadcast_clamp_fusion), kind=kCustom, calls=%fused_computation.3 | custom fusion | bytes 16785408 | tf_op jit(solution)/shard_map/gather | solution.py:74
  268.9 14.9 %all-to-all-start.2 = ((bf16[8,256,2048]{2,1,0:T(8,128)(2,1)}), bf16[8,256,2048]{2,1,0:T(8,128)(2,1)}, u32[]{:S(2)}, u32[]{:S(2)}) async-start(bf16[8,256,2048]{2,1,0:T(8,128)(2,1)} %bitcast.64), calls=%async_computation.2 | async-start | bytes 16777216 | tf_op jit(solution)/shard_map/all_to_all | solution.py:75
  283.8 0.1 copy.32
  283.9 0.1 reshape.495
  284.0 4.5 %gather_fusion.4 = s32[1024]{0:T(1024)S(1)} fusion(s32[1024]{0:T(1024)S(1)} %reshape.421, s32[1024]{0:T(1024)S(1)} %get-tuple-element.23), kind=kCustom, calls=%fused_computation.4 | custom fusion | bytes 12288 | tf_op jit(solution)/shard_map/gather | solution.py:27
  288.6 0.3 fusion.28
  288.9 7.0 %gather_fusion.6 = f32[1024]{0:T(1024)S(1)} fusion(f32[128,64]{0,1:T(8,128)S(1)} %fusion.5, s32[1024]{0:T(1024)S(1)} %reshape.495), kind=kCustom, calls=%fused_computation.6 | custom fusion | bytes 16384 | tf_op jit(solution)/shard_map/jit(take_along_axis)/gather | solution.py:66
  296.1 0.1 copy.34
  296.2 0.7 fusion.27
  296.9 4.4 %compare_select_fusion.11 = (s32[1024,1]{0,1:T(1,128)S(1)}, s32[1024,1]{0,1:T(1,128)S(1)}) fusion(s32[]{:T(128)} %bitcast.19, s32[]{:T(128)} %bitcast.20, s32[]{:T(128)} %bitcast.21, s32[]{:T(128)} %bitcast.22, s32[]{:T(128)} %bitcast.23, s32[]{:T(128)} %bitcast.25, s32[]{:T(128)} %bitcast.24, s32[1024,1]{0,1:T(1,128)S(1)} %bitcast.69), kind=kLoop, calls=%fused_computation.40 | loop fusion | flops 30720 | bytes 12316 | tf_op jit(solution)/shard_map/gather | solution.py:31
  301.4 0.7 fusion.17
  302.1 4.5 %scatter_custom_fusion.2 = s32[1024]{0:T(1024)S(1)} fusion(s32[1024]{0:T(1024)S(1)} %get-tuple-element.24, s32[1024]{0:T(1024)S(1)} %fusion.17, s32[]{:T(128)} %constant.46.clone.1), kind=kCustom, calls=%fused_computation.84 | custom fusion | bytes 4100 | tf_op jit(solution)/shard_map/scatter | solution.py:32
  306.6 70.7 %all-to-all-done.2 = bf16[8,256,2048]{2,1,0:T(8,128)(2,1)} async-done(((bf16[8,256,2048]{2,1,0:T(8,128)(2,1)}), bf16[8,256,2048]{2,1,0:T(8,128)(2,1)}, u32[]{:S(2)}, u32[]{:S(2)}) %all-to-all-start.2) | async-done | bytes 8388640 | tf_op jit(solution)/shard_map/all_to_all | solution.py:75
  377.3 13.3 %gather_fusion.5 = bf16[1024,2048]{1,0:T(8,128)(2,1)} fusion(bf16[2048,2048]{1,0:T(8,128)(2,1)} %bitcast.16, s32[1024]{0:T(1024)S(1)} %fusion.18), kind=kCustom, calls=%fused_computation.5 | custom fusion | bytes 8392704 | tf_op jit(solution)/shard_map/gather | solution.py:76
  390.7 6.5 %fusion = f32[128,2048]{1,0:T(8,128)S(1)} fusion(bf16[1024,2048]{1,0:T(8,128)(2,1)} %gather_fusion.5, f32[128,8]{1,0:T(8,128)S(1)} %copy.34), kind=kLoop, calls=%fused_computation.12 | loop fusion | flops 6029312 | bytes 5246976 | tf_op jit(solution)/shard_map/reduce_sum | solution.py:77
  397.2 0.9 fusion.4
  (44 shorter events, 0.7 us)
Async XLA Ops:
  0.0 288.6 %copy-start = (bf16[2048,64]{0,1:T(8,128)(2,1)S(1)}, bf16[2048,64]{0,1:T(8,128)(2,1)}, u32[]{:S(2)}) copy-start(bf16[2048,64]{0,1:T(8,128)(2,1)} %param.10) | copy-start | bytes 786436
  0.0 31.6 %copy-start.1 = (bf16[128,2048]{1,0:T(8,128)(2,1)S(1)}, bf16[128,2048]{1,0:T(8,128)(2,1)}, u32[]{:S(2)}) copy-start(bf16[128,2048]{1,0:T(8,128)(2,1)} %param.7) | copy-start | bytes 1572868
  9.3 33.6 %all-to-all-start.1 = ((s32[8,1,8]{2,1,0:T(1,128)}), s32[8,1,8]{2,1,0:T(1,128)S(1)}, u32[]{:S(2)}, u32[]{:S(2)}) async-start(s32[8,1,8]{2,1,0:T(1,128)} %bitcast.1), calls=%async_computation.1 | async-start | bytes 8192 | tf_op jit(solution)/shard_map/all_to_all | solution.py:69
  42.9 98.5 %all-to-all-start = ((bf16[8,256,2048]{2,1,0:T(8,128)(2,1)}), bf16[8,256,2048]{2,1,0:T(8,128)(2,1)}, u32[]{:S(2)}, u32[]{:S(2)}) async-start(bf16[8,256,2048]{2,1,0:T(8,128)(2,1)} %bitcast.65), calls=%async_computation | async-start | bytes 16777216 | tf_op jit(solution)/shard_map/all_to_all | solution.py:70
  268.9 14.9 %copy-start.3 = (s32[128,8]{0,1:T(8,128)S(1)}, s32[128,8]{0,1:T(8,128)}, u32[]{:S(2)}) copy-start(s32[128,8]{0,1:T(8,128)} %param.8) | copy-start | bytes 12292
  268.9 108.4 %all-to-all-start.2 = ((bf16[8,256,2048]{2,1,0:T(8,128)(2,1)}), bf16[8,256,2048]{2,1,0:T(8,128)(2,1)}, u32[]{:S(2)}, u32[]{:S(2)}) async-start(bf16[8,256,2048]{2,1,0:T(8,128)(2,1)} %bitcast.64), calls=%async_computation.2 | async-start | bytes 16777216 | tf_op jit(solution)/shard_map/all_to_all | solution.py:75
  377.3 19.9 %copy-start.2 = (bf16[128,2048]{1,0:T(8,128)(2,1)S(1)}, bf16[128,2048]{1,0:T(8,128)(2,1)}, u32[]{:S(2)}) copy-start(bf16[128,2048]{1,0:T(8,128)(2,1)} %param.7) | copy-start | bytes 1572868
where the time goes:
time: 402 us; the launch traced here: 398 us
  waiting for transfers between devices  143 us (36%)
  local copies, waits for them, and re-layouts  106 us (26%)
  Pallas kernels  77 us (19%)
  other arithmetic  45.4 us (11%)
  starting transfers between devices  25.9 us (6%)
    another operation x3, Pallas kernels  75.5 us
    all_to_all x1, waiting for transfers between devices, device_step(): recv_rows = lax.all_to_all(send_rows, 'ep', 0, 0, tiled=True)  72.1 us
    all_to_all x1, waiting for transfers between devices, device_step(): home_rows = lax.all_to_all(back_rows, 'ep', 0, 0, tiled=True)  70.7 us
    gather x1, local copies, waits for them, and re-layouts, device_step(): back_rows = expert_out[back_pos].reshape(ep_size, send_max, width)  19.9 us
    gather x1, local copies, waits for them, and re-layouts, device_step(): compact_rows = recv_rows.reshape(ep_size * send_max, width)[compact_src]  17.1 us
    all_to_all x1, starting transfers between devices, device_step(): home_rows = lax.all_to_all(back_rows, 'ep', 0, 0, tiled=True)  14.9 us
    gather x1, local copies, waits for them, and re-layouts, device_step(): home_rows.reshape(ep_size * send_max, width)[slot_of_pair]  13.3 us
    gather x1, local copies, waits for them, and re-layouts, device_step(): send_rows = normed[send_tok].reshape(ep_size, send_max, width)  11 us
  transfers between devices with their start and end apart: 3, of which 2 were waited for; matrix products, arithmetic and copies ran while one was open for 18% of the time, Pallas kernels for 0%

commit v1 on v0

v1 whole, which is shorter than its diff:
```python
import functools

import jax
import jax.numpy as jnp
from jax import lax
from jax.experimental import pallas as pl
from jax.experimental.pallas import tpu as pltpu
from jax.sharding import PartitionSpec as P

NORM_EPS = 1e-5
BR = 128
WIN = 256
ALIGN = 16
CW = 256
LAG = 5
F32 = jnp.float32
BF16 = jnp.bfloat16
MESH = pl.DeviceIdType.MESH
ANY = pl.BlockSpec(memory_space=pl.ANY)
VM = pl.BlockSpec(memory_space=pltpu.VMEM)
SM = pl.BlockSpec(memory_space=pltpu.SMEM)


def ring_ids(n_dev):
    me = lax.axis_index('ep')
    n_chip = n_dev // 2
    chip, core = me // 2, me % 2
    right = ((chip + 1) % n_chip) * 2 + core
    left = ((chip + n_chip - 1) % n_chip) * 2 + core
    partner = chip * 2 + (1 - core)
    return me, chip, core, right, left, partner


def enter(peers):
    barrier = pltpu.get_barrier_semaphore()
    for peer in peers:
        pl.semaphore_signal(barrier, inc=1, device_id={'ep': peer}, device_id_type=MESH)
    return lambda: pl.semaphore_wait(barrier, len(peers))


def dispatch_kernel(n_dev, nb, x_ref, g_ref, wr_ref, ids_ref, xs_out, pt_out, gb_out, tab_out,
                    u, p, xs, pt, gb, tab, ids, posm, ids_ssem, ids_rsem, ssem, rsem, osem):
    me, chip, core, right, left, partner = ring_ids(n_dev)
    n_chip = n_dev // 2
    tok = x_ref.shape[0]
    half = tok // 2
    e_local = 8
    opp = (chip + 2) % n_chip
    others = [(me + i) % n_dev for i in range(1, n_dev)]
    wait_entry = enter(others)

    gain = g_ref[...].astype(F32)
    step = tok // 4
    for i in range(4):
        x32 = x_ref[i * step:(i + 1) * step, :].astype(F32)
        inv = lax.rsqrt(jnp.mean(x32 * x32, axis=1, keepdims=True) + NORM_EPS)
        u[me, i * step:(i + 1) * step, :] = (x32 * inv * gain).astype(BF16)
    wait_entry()

    for i, peer in enumerate(others):
        pltpu.make_async_remote_copy(ids_ref, ids.at[me], ids_ssem.at[i], ids_rsem.at[me],
                                     device_id={'ep': peer}, device_id_type=MESH).start()

    def send(i, blk, h, peer):
        ref = u.at[blk, pl.ds(h * half, half), :]
        return pltpu.make_async_remote_copy(ref, ref, ssem.at[i], rsem.at[blk, h],
                                            device_id={'ep': peer}, device_id_type=MESH)

    sends = [send(0, me, 0, right), send(1, me, 1, left), send(2, me, 0, partner), send(3, me, 1, partner),
             send(4, me, 1, right), send(5, me, 0, left)]
    for s in sends:
        s.start()

    def arrived(blk, h):
        send(0, blk, h, partner).wait_recv()

    def forward(i, blk, h, peer):
        s = send(i, blk, h, peer)
        s.start()
        sends.append(s)

    ids[me] = ids_ref[...]
    for i in range(1, n_dev):
        src = (me + i) % n_dev
        pltpu.make_async_remote_copy(ids_ref, ids.at[src], ids_ssem.at[0], ids_rsem.at[src],
                                     device_id={'ep': partner}, device_id_type=MESH).wait_recv()
    sub = lax.broadcasted_iota(jnp.int32, (e_local, tok), 0)
    gid = sub + me * e_local
    hits = []
    for s in range(n_dev):
        hit = jnp.zeros((e_local, tok), jnp.int32)
        for j in range(ids_ref.shape[0]):
            hit = hit + (ids[s, j:j + 1, :] == gid).astype(jnp.int32)
        hits.append(hit.astype(F32))
    hit_all = jnp.concatenate(hits, axis=0).astype(BF16)
    ri = lax.broadcasted_iota(jnp.int32, (tok, tok), 0)
    ci = lax.broadcasted_iota(jnp.int32, (tok, tok), 1)
    before = (ri < ci).astype(F32).astype(BF16)
    cnt_all = jnp.dot(hit_all, jnp.ones((tok, tok), BF16), preferred_element_type=F32)
    rank_all = jnp.dot(hit_all, before, preferred_element_type=F32)
    total = jnp.zeros((e_local, tok), F32)
    for s in range(n_dev):
        total = total + cnt_all[s * e_local:(s + 1) * e_local, :]
    blocks = jnp.floor((total + (BR - 1)) * (1.0 / BR))
    first = jnp.zeros((e_local, tok), F32)
    for e in range(e_local - 1):
        first = first + jnp.where(sub > e, jnp.broadcast_to(blocks[e:e + 1, :], (e_local, tok)), 0.0)
    last = first + blocks
    lane = lax.broadcasted_iota(jnp.int32, (e_local, tok), 1).astype(F32)
    blk_exp = jnp.sum(jnp.where(lane >= last, 1.0, 0.0), axis=0, keepdims=True)
    tab[0:8, :] = blocks.astype(jnp.int32)
    tab[8:16, :] = first.astype(jnp.int32)
    tab[16:24, :] = jnp.broadcast_to(jnp.minimum(blk_exp, e_local - 1.0), (8, tok)).astype(jnp.int32)
    carry = jnp.zeros((e_local, tok), F32)
    wlane = lax.broadcasted_iota(jnp.int32, (tok, WIN), 1).astype(F32)
    for s in range(n_dev):
        run = first * BR + carry
        pos = run + rank_all[s * e_local:(s + 1) * e_local, :]
        start = jnp.floor(run * (1.0 / ALIGN)) * ALIGN
        tab[24 + s * 8:32 + s * 8, :] = (start * (1.0 / ALIGN)).astype(jnp.int32)
        rel = jnp.where(hits[s] > 0, pos - start, -1.0)
        posm[s * 8:(s + 1) * 8, :] = jnp.where(hits[s] > 0, pos + 1.0, 0.0)
        rel_t = jnp.concatenate([rel, jnp.zeros((tok - e_local, tok), F32)], axis=0).T
        par = (s % 2 + core + 1) % 2
        for e in range(e_local):
            col = jnp.broadcast_to(rel_t[:, e:e + 1], (tok, WIN))
            pt[par, s // 2, e] = jnp.where(col == wlane, 1.0, 0.0).astype(BF16)
        carry = carry + cnt_all[s * e_local:(s + 1) * e_local, :]
    row_i = lax.broadcasted_iota(jnp.int32, (BR, tok), 0).astype(F32)

    @pl.loop(0, nb)
    def _(b):
        bf = b.astype(F32)
        mine = (first <= bf) & (bf < last)
        for s in range(n_dev):
            sel = jnp.sum(jnp.where(mine, posm[s * 8:(s + 1) * 8, :], 0.0), axis=0, keepdims=True) - (1.0 + BR * bf)
            p[s // 2, pl.ds(pl.multiple_of(b * BR, BR), BR), (s % 2) * tok:(s % 2 + 1) * tok] = jnp.where(
                jnp.broadcast_to(sel, (BR, tok)) == row_i, 1.0, 0.0).astype(BF16)

    tab_copy = pltpu.make_async_copy(tab, tab_out, osem.at[0])
    tab_copy.start()
    pt_copy = pltpu.make_async_copy(pt, pt_out, osem.at[1])
    pt_copy.start()

    def gates(c):
        for k in range(2):
            blk = c * 2 + k
            logits = jnp.dot(u[blk], wr_ref[...], preferred_element_type=F32)
            ex = jnp.exp(logits - jnp.max(logits, axis=1, keepdims=True))
            prob = ex / jnp.sum(ex, axis=1, keepdims=True)
            par = (k + core + 1) % 2
            for e in range(e_local):
                gb[par, c, e] = jnp.broadcast_to(prob[:, e:e + 1], (tok, 128))

    width = u.shape[2]
    nt = 512

    def gather(c, first_pass):
        @pl.loop(0, nb)
        def _(b):
            rows = pl.ds(pl.multiple_of(b * BR, BR), BR)
            pb = p[c, rows, :]
            for n in range(width // nt):
                uc = jnp.concatenate([u[c * 2, :, n * nt:(n + 1) * nt], u[c * 2 + 1, :, n * nt:(n + 1) * nt]], axis=0)
                part = jnp.dot(pb, uc, preferred_element_type=F32).astype(BF16)
                if first_pass:
                    xs[rows, n * nt:(n + 1) * nt] = part
                else:
                    xs[rows, n * nt:(n + 1) * nt] = xs[rows, n * nt:(n + 1) * nt] + part

    arrived(left, 0)
    forward(6, left, 0, right)
    arrived(right, 1)
    forward(7, right, 1, left)
    forward(8, left, 0, partner)
    forward(9, right, 1, partner)
    arrived(partner, 0)
    arrived(partner, 1)
    gates(chip)
    gather(chip, True)
    arrived(left, 1)
    forward(10, left, 1, partner)
    arrived(right, 0)
    forward(11, right, 0, partner)
    lchip, rchip = (chip + n_chip - 1) % n_chip, (chip + 1) % n_chip
    for blk in (lchip * 2 + (1 - core), rchip * 2 + (1 - core)):
        arrived(blk, 0)
        arrived(blk, 1)
    gates(lchip)
    gather(lchip, False)
    oblk = opp * 2 + core
    arrived(oblk, 0)
    forward(12, oblk, 0, partner)
    arrived(oblk, 1)
    forward(13, oblk, 1, partner)
    gates(rchip)
    gather(rchip, False)
    arrived(opp * 2 + (1 - core), 0)
    arrived(opp * 2 + (1 - core), 1)
    gates(opp)
    gb_copy = pltpu.make_async_copy(gb, gb_out, osem.at[2])
    gb_copy.start()
    gather(opp, False)
    xs_copy = pltpu.make_async_copy(xs, xs_out, osem.at[3])
    xs_copy.start()
    for s in sends:
        s.wait_send()
    for i, peer in enumerate(others):
        pltpu.make_async_remote_copy(ids_ref, ids.at[me], ids_ssem.at[i], ids_rsem.at[me],
                                     device_id={'ep': peer}, device_id_type=MESH).wait_send()
    for cp in (tab_copy, pt_copy, gb_copy, xs_copy):
        cp.wait()


def hidden_kernel(nb, slots, ft, tab, xs_hbm, w1_hbm, w3_hbm, h_out, xs, w1, w3, h, xsem, wsem, hsem):
    e_local = w1_hbm.shape[0]
    ff = w1_hbm.shape[2]
    parts = ff // ft
    steps = e_local * parts
    used = tab[15, 0] + tab[7, 0]

    def wcopy(n):
        e, f = n // parts, n % parts
        slot = n % slots
        cols = pl.ds(pl.multiple_of(f * ft, ft), ft)
        return (pltpu.make_async_copy(w1_hbm.at[e, :, cols], w1.at[slot], wsem.at[0, slot]),
                pltpu.make_async_copy(w3_hbm.at[e, :, cols], w3.at[slot], wsem.at[1, slot]))

    def xcopy(b):
        rows = pl.ds(pl.multiple_of(b * BR, BR), BR)
        return pltpu.make_async_copy(xs_hbm.at[rows, :], xs.at[rows, :], xsem.at[b])

    for cp in wcopy(0):
        cp.start()

    @pl.loop(0, used)
    def _(b):
        xcopy(b).start()

    for n in range(1, slots):
        for cp in wcopy(n):
            cp.start()

    @pl.loop(used, nb)
    def _(b):
        h[pl.ds(pl.multiple_of(b * BR, BR), BR), :] = jnp.zeros((BR, ff), BF16)

    @pl.loop(0, steps)
    def _(n):
        e, f, slot = n // parts, n % parts, n % slots
        for cp in wcopy(n):
            cp.wait()
        first = tab[8 + e, 0]

        @pl.loop(first, first + tab[e, 0])
        def _(b):
            @pl.when(f == 0)
            def _():
                xcopy(b).wait()
            rows = pl.ds(pl.multiple_of(b * BR, BR), BR)
            xb = xs[rows, :]
            hg = jnp.dot(xb, w1[slot], preferred_element_type=F32)
            hu = jnp.dot(xb, w3[slot], preferred_element_type=F32)
            h[rows, pl.ds(pl.multiple_of(f * ft, ft), ft)] = (hg * jax.nn.sigmoid(hg) * hu).astype(BF16)

        @pl.when(n + slots < steps)
        def _():
            for cp in wcopy(n + slots):
                cp.start()

    out = pltpu.make_async_copy(h, h_out, hsem)
    out.start()
    out.wait()


def return_kernel(n_dev, nb, chunks, tab, x_ref, h_hbm, w2_hbm, pt_hbm, gb_hbm, o_ref,
                  h, w2a, w2b, pt, gb, o, dsend, drecv, z, r1, rd, r2, s2,
                  insem, wsem, d_ss, d_rs, s1_ss, r1_rs, rd_rs, s2_ss, r2_rs):
    me, chip, core, right, left, partner = ring_ids(n_dev)
    n_chip = n_dev // 2
    tok = x_ref.shape[0]
    half = tok // 2
    e_local = w2_hbm.shape[0]
    wait_entry = enter([right, left, partner])

    w2s = (w2a, w2b)

    def wcopy(k, i):
        return pltpu.make_async_copy(w2_hbm.at[:, :, pl.ds(pl.multiple_of(k * CW, CW), CW)], w2s[i], wsem.at[i])

    h_in = pltpu.make_async_copy(h_hbm, h, insem.at[0])
    h_in.start()
    wcopy(0, 0).start()
    pt_in = pltpu.make_async_copy(pt_hbm, pt, insem.at[1])
    pt_in.start()
    gb_in = pltpu.make_async_copy(gb_hbm, gb, insem.at[2])
    gb_in.start()
    o[nb * BR // ALIGN:] = jnp.zeros((o.shape[0] - nb * BR // ALIGN, ALIGN, CW), BF16)
    wait_entry()
    h_in.wait()

    lo, hi = pl.ds(0, half), pl.ds(half, half)
    rc, lc, oc = (chip + 1) % n_chip, (chip + n_chip - 1) % n_chip, (chip + 2) % n_chip

    def rcopy(src, dst, ss, rs, peer):
        return pltpu.make_async_remote_copy(src, dst, ss, rs, device_id={'ep': peer}, device_id_type=MESH)

    def pair_copy(k):
        return rcopy(dsend.at[k], drecv.at[k], d_ss.at[k], d_rs.at[k], partner)

    def s1_copies(k):
        return (rcopy(z.at[k, oc, lo, :], r1.at[k, 0], s1_ss.at[k, 0], r1_rs.at[k, 0], right),
                rcopy(z.at[k, oc, hi, :], r1.at[k, 1], s1_ss.at[k, 1], r1_rs.at[k, 1], left),
                rcopy(z.at[k, lc, lo, :], rd.at[k, 0], s1_ss.at[k, 2], rd_rs.at[k, 0], left),
                rcopy(z.at[k, rc, hi, :], rd.at[k, 1], s1_ss.at[k, 3], rd_rs.at[k, 1], right))

    def s2_copies(k):
        return (rcopy(s2.at[k, 0], r2.at[k, 0], s2_ss.at[k, 0], r2_rs.at[k, 0], right),
                rcopy(s2.at[k, 1], r2.at[k, 1], s2_ss.at[k, 1], r2_rs.at[k, 1], left))

    def combine(par, d):
        s = d * 2 + (core if par == 1 else 1 - core)
        acc = jnp.zeros((tok, CW), F32)
        for e in range(e_local):
            win = o[pl.ds(tab[24 + s * 8 + e, 0], WIN // ALIGN)].reshape(WIN, CW)
            m = jnp.dot(pt[par, d, e], win, preferred_element_type=F32)
            g = gb[par, d, e]
            acc = acc + jnp.concatenate([g] * (CW // 128), axis=1) * m
        return acc

    def one_step(k, i):
        @pl.when((k >= 5) & (k < chunks + 5))
        def _():
            kk = k - 5
            r2c, s1c = s2_copies(kk), s1_copies(kk)
            cols = pl.ds(pl.multiple_of(kk * CW, CW), CW)
            for i, rows in enumerate((lo, hi)):
                r2c[i].wait_recv()
                s1c[2 + i].wait_recv()
                tot = z[kk, chip, rows, :] + r2[kk, i] + rd[kk, i] + x_ref[rows, cols].astype(F32)
                o_ref[rows, cols] = tot.astype(BF16)

        @pl.when((k >= 3) & (k < chunks + 3))
        def _():
            kk = k - 3
            s1c, s2c = s1_copies(kk), s2_copies(kk)
            s1c[0].wait_recv()
            s2[kk, 0] = r1[kk, 0] + z[kk, rc, lo, :]
            s2c[0].start()
            s1c[1].wait_recv()
            s2[kk, 1] = r1[kk, 1] + z[kk, lc, hi, :]
            s2c[1].start()

        @pl.when(k < chunks)
        def _():
            wcopy(k, i).wait()

            @pl.when(k + 1 < chunks)
            def _():
                wcopy(k + 1, 1 - i).start()
            for b in range(nb):
                hb = h[b * BR:(b + 1) * BR, :]
                ob = jnp.dot(hb, w2s[i][tab[16, b]], preferred_element_type=F32).astype(BF16)
                o[b * BR // ALIGN:(b + 1) * BR // ALIGN] = ob.reshape(BR // ALIGN, ALIGN, CW)

        @pl.when((k >= 1) & (k < chunks + 1))
        def _():
            kk = k - 1
            pair_copy(kk).wait_recv()
            for d in range(n_chip):
                z[kk, d] = z[kk, d] + drecv[kk, d]
            for cp in s1_copies(kk):
                cp.start()

        @pl.when(k < chunks)
        def _():
            @pl.when(k == 0)
            def _():
                pt_in.wait()
                gb_in.wait()
            for d in range(n_chip):
                dsend[k, d] = combine(0, d)
            pair_copy(k).start()
            for d in range(n_chip):
                z[k, d] = combine(1, d)

    @pl.loop(0, (chunks + LAG + 1) // 2)
    def _(k2):
        one_step(k2 * 2, 0)
        one_step(k2 * 2 + 1, 1)

    @pl.loop(0, chunks)
    def _(k):
        pair_copy(k).wait_send()
        for cp in s1_copies(k) + s2_copies(k):
            cp.wait_send()


def solution(mesh):
    n_dev = mesh.shape['ep']

    def device_step(tokens, expert_ids, norm_gain, w_router, w_gate, w_up, w_down):
        tok, top_k = expert_ids.shape
        width = tokens.shape[1]
        e_local, _, ff = w_gate.shape
        n_chip = n_dev // 2
        recv_max = 3 * tok * top_k // 2
        nb = (recv_max - e_local) // BR + e_local
        rows = nb * BR
        chunks = width // CW
        me = lax.axis_index('ep')
        wr = jnp.roll(w_router, -me * e_local, axis=1)
        ids_t = expert_ids.T
        dma = pltpu.SemaphoreType.DMA
        params = lambda **kw: pltpu.CompilerParams(vmem_limit_bytes=60 * 1024 * 1024, **kw)

        xs, pt, gb, tab = pl.pallas_call(
            functools.partial(dispatch_kernel, n_dev, nb),
            name='dispatch',
            out_shape=(jax.ShapeDtypeStruct((rows, width), BF16),
                       jax.ShapeDtypeStruct((2, n_chip, e_local, tok, WIN), BF16),
                       jax.ShapeDtypeStruct((2, n_chip, e_local, tok, 128), F32),
                       jax.ShapeDtypeStruct((24 + n_dev * 8, 128), jnp.int32)),
            in_specs=[VM] * 4,
            out_specs=(ANY,) * 4,
            scratch_shapes=[pltpu.VMEM((n_dev, tok, width), BF16),
                            pltpu.VMEM((n_chip, rows, 2 * tok), BF16),
                            pltpu.VMEM((rows, width), BF16),
                            pltpu.VMEM((2, n_chip, e_local, tok, WIN), BF16),
                            pltpu.VMEM((2, n_chip, e_local, tok, 128), F32),
                            pltpu.VMEM((24 + n_dev * 8, 128), jnp.int32),
                            pltpu.VMEM((n_dev, top_k, tok), jnp.int32),
                            pltpu.VMEM((n_dev * 8, tok), F32),
                            dma((n_dev - 1,)), dma((n_dev,)), dma((14,)), dma((n_dev, 2)), dma((4,))],
            compiler_params=params(collective_id=0, has_side_effects=True),
        )(tokens, norm_gain.reshape(1, width), wr, ids_t)

        slots, ft = 3, 512
        h = pl.pallas_call(
            functools.partial(hidden_kernel, nb, slots, ft),
            name='hidden',
            out_shape=jax.ShapeDtypeStruct((rows, ff), BF16),
            in_specs=[SM, ANY, ANY, ANY],
            out_specs=ANY,
            scratch_shapes=[pltpu.VMEM((rows, width), BF16),
                            pltpu.VMEM((slots, width, ft), BF16),
                            pltpu.VMEM((slots, width, ft), BF16),
                            pltpu.VMEM((rows, ff), BF16),
                            dma((nb,)), dma((2, slots)), dma(())],
            compiler_params=params(),
        )(tab, xs, w_gate, w_up)

        blk = (chunks, 2, tok // 2, CW)
        out = pl.pallas_call(
            functools.partial(return_kernel, n_dev, nb, chunks),
            name='return',
            out_shape=jax.ShapeDtypeStruct((tok, width), BF16),
            in_specs=[SM, VM, ANY, ANY, ANY, ANY],
            out_specs=VM,
            scratch_shapes=[pltpu.VMEM((rows, ff), BF16),
                            pltpu.VMEM((e_local, ff, CW), BF16),
                            pltpu.VMEM((e_local, ff, CW), BF16),
                            pltpu.VMEM((2, n_chip, e_local, tok, WIN), BF16),
                            pltpu.VMEM((2, n_chip, e_local, tok, 128), F32),
                            pltpu.VMEM(((rows + WIN) // ALIGN, ALIGN, CW), BF16),
                            pltpu.VMEM((chunks, n_chip, tok, CW), F32),
                            pltpu.VMEM((chunks, n_chip, tok, CW), F32),
                            pltpu.VMEM((chunks, n_chip, tok, CW), F32),
                            pltpu.VMEM(blk, F32), pltpu.VMEM(blk, F32), pltpu.VMEM(blk, F32), pltpu.VMEM(blk, F32),
                            dma((3,)), dma((2,)), dma((chunks,)), dma((chunks,)),
                            dma((chunks, 4)), dma((chunks, 2)), dma((chunks, 2)), dma((chunks, 2)), dma((chunks, 2))],
            compiler_params=params(collective_id=1, has_side_effects=True),
        )(tab, tokens, h, w_down, pt, gb)
        return out

    row_spec = P(('dp', 'ep'), None)
    expert_spec = P('ep', None, None)
    return jax.shard_map(device_step, mesh=mesh, in_specs=(row_spec, row_spec, P(None), P(None, None), expert_spec, expert_spec, expert_spec), out_specs=row_spec, check_vma=False)
```

time: 402 us -> 134 us (0.33)
  the two profiles are of different devices: /device:TPU:81 before, /device:TPU:88 now
where the time goes in v1:
time: 134 us; the launch traced here: 135 us
  Pallas kernels  129 us (96%)
  local copies, waits for them, and re-layouts  4.38 us (3%)
  other arithmetic  1.35 us (1%)
    pallas_call x1, Pallas kernels, device_step(): pl.pallas_call(functools.partial(return_kernel, n_dev, nb, chunks), name=...  55.1 us
    pallas_call x1, Pallas kernels, device_step(): pl.pallas_call(functools.partial(dispatch_kernel, n_dev, nb), name='dispa...  45.8 us
    pallas_call x1, Pallas kernels, device_step(): pl.pallas_call(functools.partial(hidden_kernel, nb, slots, ft), name='hid...  27.9 us
    unnamed x2, local copies, waits for them, and re-layouts  3.1 us

profile of v1, /device:TPU:88, one launch (start us, length us, event | category | flops | bytes accessed | tf_op | source)
XLA Modules:
  0.0 134.6 jit_solution(16061560915971107689)
XLA Ops:
  0.0 1.3 reshape.3.g_ref
  1.3 1.2 copy.8
  2.5 1.4 %dynamic-slice_maximum_fusion.wr_ref = bf16[2048,64]{1,0:T(8,128)(2,1)} fusion(s32[]{:T(128)S(6)} %select_n.14, bf16[2048,64]{1,0:T(8,128)(2,1)S(1)} %copy.8), kind=kLoop, calls=%fused_computation | loop fusion | flops 524288 | bytes 524292 | tf_op jit(solution)/shard_map/jit(_roll_dynamic)/concatenate | solution.py:412
  3.9 45.8 %dispatch.1 = (bf16[2432,2048]{1,0:T(8,128)(2,1)}, bf16[2,4,8,128,256]{4,3,2,1,0:T(8,128)(2,1)}, f32[2,4,8,128,128]{4,3,2,1,0:T(8,128)}, s32[88,128]{1,0:T(8,128)}) custom-call(bf16[128,2048]{1,0:T(8,128)(2,1)} %x_ref.3, bf16[1,2048]{1,0:T(2,128)(2,1)} %reshape.3.g_ref, bf16[2048,64]{1,0:T(8,128)(2,1)} %dynamic-slice_maximum_fusion.wr_ref, s32[8,128]{1,0:T(8,128)} %bitcast.1), custom_call_target="tpu_custom_call" | custom-call | tf_op jit(solution)/shard_map/dispatch/pallas_call | solution.py:417
  49.7 27.9 %hidden.1.h_hbm = bf16[2432,1024]{1,0:T(8,128)(2,1)} custom-call(s32[88,128]{1,0:T(8,128)} %get-tuple-element.9.tab, bf16[2432,2048]{1,0:T(8,128)(2,1)} %get-tuple-element.10.xs_hbm, bf16[8,2048,1024]{2,1,0:T(8,128)(2,1)} %w1_hbm.1, bf16[8,2048,1024]{2,1,0:T(8,128)(2,1)} %w3_hbm.1), custom_call_target="tpu_custom_call" | custom-call | tf_op jit(solution)/shard_map/hidden/pallas_call | solution.py:439
  77.6 55.1 %return.1 = bf16[128,2048]{1,0:T(8,128)(2,1)} custom-call(s32[88,128]{1,0:T(8,128)} %get-tuple-element.9.tab, bf16[128,2048]{1,0:T(8,128)(2,1)} %x_ref.3, bf16[2432,1024]{1,0:T(8,128)(2,1)} %hidden.1.h_hbm, bf16[8,1024,2048]{2,1,0:T(8,128)(2,1)} %w2_hbm.1, bf16[2,4,8,128,256]{4,3,2,1,0:T(8,128)(2,1)} %get-tuple-element.11.pt_hbm, ...), custom_call_target="tpu_custom_call" | custom-call | tf_op jit(solution)/shard_map/return/pallas_call | solution.py:454
  132.7 1.9 %copy.11 = bf16[128,2048]{1,0:T(8,128)(2,1)} copy(bf16[128,2048]{1,0:T(8,128)(2,1)} %return.1) | data formatting | bytes 1048576

commit v2 on v0

v2 whole, which is shorter than its diff:
```python
import functools

import jax
import jax.numpy as jnp
from jax import lax
from jax.experimental import pallas as pl
from jax.experimental.pallas import tpu as pltpu
from jax.sharding import PartitionSpec as P

NORM_EPS = 1e-5
BR = 128
WIN = 256
ALIGN = 16
FC = 128
CW = 256
LAG = 5
F32 = jnp.float32
BF16 = jnp.bfloat16
I32 = jnp.int32
MESH = pl.DeviceIdType.MESH
ANY = pl.BlockSpec(memory_space=pl.ANY)
VM = pl.BlockSpec(memory_space=pltpu.VMEM)


def moe_kernel(n_dev, nb, chunks, x_ref, ids_ref, g_ref, wr_ref, w1_hbm, w3_hbm, w2_hbm, o_ref,
               u, wb0, wb1, h, pt, gb, ids, posm, tab_v, tab, drecv, r1, rd, r2,
               wsem, tsem, ids_ssem, ids_rsem, ssem, rsem,
               d_ss, d_rs, s1_ss, r1_rs, rd_rs, s2_ss, r2_rs):
    n_chip = n_dev // 2
    tok, width = x_ref.shape
    half = tok // 2
    top_k = ids_ref.shape[0]
    e_local, ff = w2_hbm.shape[0], w2_hbm.shape[1]
    rows = nb * BR
    f_steps = ff // FC
    wbs = (wb0, wb1)

    def rcopy(src, dst, ss, rs, peer):
        return pltpu.make_async_remote_copy(src, dst, ss, rs, device_id={'ep': peer}, device_id_type=MESH)

    def expert_of(b):
        return jnp.minimum(jnp.maximum(tab[0, b], 0), e_local - 1)

    def window_of(s, e):
        return jnp.minimum(jnp.maximum(tab[8 + s * 8 + e, 0], 0), rows // ALIGN)

    def coords():
        me = lax.axis_index('ep')
        chip, core = me // 2, me % 2
        rc, lc, oc = (chip + 1) % n_chip, (chip + n_chip - 1) % n_chip, (chip + 2) % n_chip
        return me, chip, core, rc, lc, oc, rc * 2 + core, lc * 2 + core, chip * 2 + (1 - core)

    def hidden_copies(f, i):
        cols = pl.ds(pl.multiple_of(f * FC, FC), FC)
        return (pltpu.make_async_copy(w1_hbm.at[:, :, cols], wbs[i].at[:, :, 0:FC], wsem.at[0, i]),
                pltpu.make_async_copy(w3_hbm.at[:, :, cols], wbs[i].at[:, :, FC:2 * FC], wsem.at[1, i]))

    def down_copy(k, i):
        return pltpu.make_async_copy(w2_hbm.at[:, :, pl.ds(pl.multiple_of(k * CW, CW), CW)],
                                     wbs[i].at[:, 0:ff, :], wsem.at[2, i])

    def dispatch(p, xs):
        me, chip, core, rc, lc, oc, right, left, partner = coords()
        others = [(me + i) % n_dev for i in range(1, n_dev)]
        barrier = pltpu.get_barrier_semaphore()
        for peer in others:
            pl.semaphore_signal(barrier, inc=1, device_id={'ep': peer}, device_id_type=MESH)

        for i in range(2):
            for cp in hidden_copies(i, i):
                cp.start()

        gain = g_ref[...].astype(F32).reshape(1, width)
        step = tok // 4
        for i in range(4):
            x32 = x_ref[i * step:(i + 1) * step, :].astype(F32)
            inv = lax.rsqrt(jnp.mean(x32 * x32, axis=1, keepdims=True) + NORM_EPS)
            u[chip, pl.ds(pl.multiple_of(core * tok + i * step, step), step), :] = (x32 * inv * gain).astype(BF16)
        pl.semaphore_wait(barrier, n_dev - 1)

        def send(i, blk, hf, peer):
            ref = u.at[blk // 2, pl.ds(pl.multiple_of((blk % 2) * tok + hf * half, half), half), :]
            return rcopy(ref, ref, ssem.at[i], rsem.at[blk, hf], peer)

        def ids_send(i, peer):
            return rcopy(ids_ref, ids.at[me], ids_ssem.at[i], ids_rsem.at[me], peer)

        for i, peer in enumerate(others):
            ids_send(i, peer).start()
        sends = [send(0, me, 0, right), send(1, me, 1, left), send(2, me, 0, partner), send(3, me, 1, partner),
                 send(4, me, 1, right), send(5, me, 0, left)]
        for s in sends:
            s.start()

        def arrived(blk, hf):
            send(0, blk, hf, partner).wait_recv()

        def forward(i, blk, hf, peer):
            s = send(i, blk, hf, peer)
            s.start()
            sends.append(s)

        ids[me] = ids_ref[...]
        for i in range(1, n_dev):
            src = (me + i) % n_dev
            rcopy(ids_ref, ids.at[src], ids_ssem.at[0], ids_rsem.at[src], partner).wait_recv()
        sub = lax.broadcasted_iota(I32, (e_local, tok), 0)
        gid = sub + me * e_local
        hits = []
        for s in range(n_dev):
            hit = jnp.zeros((e_local, tok), I32)
            for j in range(top_k):
                hit = hit + (ids[s, j:j + 1, :] == gid).astype(I32)
            hits.append(hit.astype(F32))
        hit_all = jnp.concatenate(hits, axis=0).astype(BF16)
        ri = lax.broadcasted_iota(I32, (tok, tok), 0)
        ci = lax.broadcasted_iota(I32, (tok, tok), 1)
        before = (ri < ci).astype(F32).astype(BF16)
        cnt_all = jnp.dot(hit_all, jnp.ones((tok, tok), BF16), preferred_element_type=F32)
        rank_all = jnp.dot(hit_all, before, preferred_element_type=F32)
        total = jnp.zeros((e_local, tok), F32)
        for s in range(n_dev):
            total = total + cnt_all[s * e_local:(s + 1) * e_local, :]
        blocks = jnp.floor((total + (BR - 1)) * (1.0 / BR))
        first = jnp.zeros((e_local, tok), F32)
        for e in range(e_local - 1):
            first = first + jnp.where(sub > e, jnp.broadcast_to(blocks[e:e + 1, :], (e_local, tok)), 0.0)
        last = first + blocks
        lane = lax.broadcasted_iota(I32, (e_local, tok), 1).astype(F32)
        blk_exp = jnp.sum(jnp.where(lane >= last, 1.0, 0.0), axis=0, keepdims=True)
        tab_v[0:8, :] = jnp.broadcast_to(jnp.minimum(blk_exp, e_local - 1.0), (8, tok)).astype(I32)
        carry = jnp.zeros((e_local, tok), F32)
        starts, rels = [], []
        for s in range(n_dev):
            run = first * BR + carry
            pos = run + rank_all[s * e_local:(s + 1) * e_local, :]
            start = jnp.floor(run * (1.0 / ALIGN))
            tab_v[8 + s * 8:16 + s * 8, :] = jnp.minimum(start, 1.0 * (rows // ALIGN)).astype(I32)
            rels.append(jnp.where(hits[s] > 0, pos - start * ALIGN, -1.0))
            posm[s * 8:(s + 1) * 8, :] = jnp.where(hits[s] > 0, pos + 1.0, 0.0)
            carry = carry + cnt_all[s * e_local:(s + 1) * e_local, :]
        tab_copy = pltpu.make_async_copy(tab_v, tab, tsem)
        tab_copy.start()
        row_i = lax.broadcasted_iota(I32, (BR, tok), 0).astype(F32)

        @pl.loop(0, nb)
        def _(b):
            bf = b.astype(F32)
            mine = (first <= bf) & (bf < last)
            for s in range(n_dev):
                sel = jnp.sum(jnp.where(mine, posm[s * 8:(s + 1) * 8, :], 0.0), axis=0, keepdims=True) - (1.0 + BR * bf)
                p[s // 2, pl.ds(pl.multiple_of(b * BR, BR), BR), (s % 2) * tok:(s % 2 + 1) * tok] = jnp.where(
                    jnp.broadcast_to(sel, (BR, tok)) == row_i, 1.0, 0.0).astype(BF16)

        def windows():
            wlane = lax.broadcasted_iota(I32, (tok, WIN), 1).astype(F32)
            for s in range(n_dev):
                rel_t = jnp.concatenate([rels[s], jnp.zeros((tok - e_local, tok), F32)], axis=0).T
                par = (s % 2 + core + 1) % 2
                for e in range(e_local):
                    col = jnp.broadcast_to(rel_t[:, e:e + 1], (tok, WIN))
                    pt[par, s // 2, e] = jnp.where(col == wlane, 1.0, 0.0).astype(BF16)

        def gates(c):
            logits = lax.dot_general(u[c], wr_ref[...], (((1,), (1,)), ((), ())), preferred_element_type=F32)
            ex = jnp.exp(logits - jnp.max(logits, axis=1, keepdims=True))
            prob = ex / jnp.sum(ex, axis=1, keepdims=True)
            full = jnp.concatenate([prob, jnp.zeros((2 * tok, 128 - prob.shape[1]), F32)], axis=1)
            mine = pltpu.roll(full, (128 - me * e_local) % 128, 1)
            for k in range(2):
                par = (k + core + 1) % 2
                for e in range(e_local):
                    gb[par, c, e] = jnp.broadcast_to(mine[k * tok:(k + 1) * tok, e:e + 1], (tok, 128))

        mt, nt = rows // 4, 256

        def gather(cs, first_pass):
            @pl.loop(0, rows // mt)
            def _(m):
                rs = pl.ds(pl.multiple_of(m * mt, mt), mt)
                for n in range(width // nt):
                    cols = slice(n * nt, (n + 1) * nt)
                    part = jnp.dot(p[cs[0], rs, :], u[cs[0], :, cols], preferred_element_type=F32)
                    for c in cs[1:]:
                        part = part + jnp.dot(p[c, rs, :], u[c, :, cols], preferred_element_type=F32)
                    if first_pass:
                        xs[rs, cols] = part.astype(BF16)
                    else:
                        xs[rs, cols] = xs[rs, cols] + part.astype(BF16)

        arrived(partner, 0)
        arrived(partner, 1)
        arrived(left, 0)
        forward(6, left, 0, right)
        arrived(right, 1)
        forward(7, right, 1, left)
        forward(8, left, 0, partner)
        forward(9, right, 1, partner)
        gather([chip], True)
        gates(chip)
        arrived(left, 1)
        forward(10, left, 1, partner)
        arrived(right, 0)
        forward(11, right, 0, partner)
        windows()
        for blk in (lc * 2 + (1 - core), rc * 2 + (1 - core)):
            arrived(blk, 0)
            arrived(blk, 1)
        gather([lc, rc], False)
        oblk = oc * 2 + core
        arrived(oblk, 0)
        forward(12, oblk, 0, partner)
        arrived(oblk, 1)
        forward(13, oblk, 1, partner)
        gates(lc)
        gates(rc)
        arrived(oc * 2 + (1 - core), 0)
        arrived(oc * 2 + (1 - core), 1)
        gather([oc], False)
        gates(oc)
        tab_copy.wait()

        @pl.loop(0, f_steps // 2)
        def _(f2):
            for i in range(2):
                f = f2 * 2 + i
                for cp in hidden_copies(f, i):
                    cp.wait()
                for b in range(nb):
                    r = jnp.dot(xs[b * BR:(b + 1) * BR, :], wbs[i][expert_of(b)], preferred_element_type=F32)
                    hg, hu = r[:, 0:FC], r[:, FC:2 * FC]
                    h[b * BR:(b + 1) * BR, pl.ds(pl.multiple_of(f * FC, FC), FC)] = (hg * jax.nn.sigmoid(hg) * hu).astype(BF16)

                @pl.when(f + 2 < f_steps)
                def _():
                    for cp in hidden_copies(f + 2, i):
                        cp.start()

                @pl.when(f + 2 >= f_steps)
                def _():
                    down_copy(i, i).start()

        for s in sends:
            s.wait_send()
        for i, peer in enumerate(others):
            ids_send(i, peer).wait_send()

    pl.run_scoped(dispatch, pltpu.VMEM((n_chip, rows, 2 * tok), BF16), pltpu.VMEM((rows, width), BF16))

    lo, hi = pl.ds(0, half), pl.ds(half, half)

    def give_back(o, dsend, z, s2):
        _, chip, core, rc, lc, oc, right, left, partner = coords()

        def pair_copy(k):
            return rcopy(dsend.at[k], drecv.at[k], d_ss.at[k], d_rs.at[k], partner)

        def s1_copies(k):
            return (rcopy(z.at[k, oc, lo, :], r1.at[k, 0], s1_ss.at[k, 0], r1_rs.at[k, 0], right),
                    rcopy(z.at[k, oc, hi, :], r1.at[k, 1], s1_ss.at[k, 1], r1_rs.at[k, 1], left),
                    rcopy(z.at[k, lc, lo, :], rd.at[k, 0], s1_ss.at[k, 2], rd_rs.at[k, 0], left),
                    rcopy(z.at[k, rc, hi, :], rd.at[k, 1], s1_ss.at[k, 3], rd_rs.at[k, 1], right))

        def s2_copies(k):
            return (rcopy(s2.at[k, 0], r2.at[k, 0], s2_ss.at[k, 0], r2_rs.at[k, 0], right),
                    rcopy(s2.at[k, 1], r2.at[k, 1], s2_ss.at[k, 1], r2_rs.at[k, 1], left))

        def combine(par, d):
            s = d * 2 + (core if par == 1 else 1 - core)
            acc = jnp.zeros((tok, CW), F32)
            for e in range(e_local):
                win = o[pl.ds(window_of(s, e), WIN // ALIGN)].reshape(WIN, CW)
                m = jnp.dot(pt[par, d, e], win, preferred_element_type=F32)
                acc = acc + jnp.concatenate([gb[par, d, e]] * (CW // 128), axis=1) * m
            return acc

        def one_step(k, i):
            @pl.when((k >= 5) & (k < chunks + 5))
            def _():
                kk = k - 5
                r2c, s1c = s2_copies(kk), s1_copies(kk)
                cols = pl.ds(pl.multiple_of(kk * CW, CW), CW)
                for j, rs in enumerate((lo, hi)):
                    r2c[j].wait_recv()
                    s1c[2 + j].wait_recv()
                    tot = z[kk, chip, rs, :] + r2[kk, j] + rd[kk, j] + x_ref[rs, cols].astype(F32)
                    o_ref[rs, cols] = tot.astype(BF16)

            @pl.when((k >= 3) & (k < chunks + 3))
            def _():
                kk = k - 3
                s1c, s2c = s1_copies(kk), s2_copies(kk)
                s1c[0].wait_recv()
                s2[kk, 0] = r1[kk, 0] + z[kk, rc, lo, :]
                s2c[0].start()
                s1c[1].wait_recv()
                s2[kk, 1] = r1[kk, 1] + z[kk, lc, hi, :]
                s2c[1].start()

            @pl.when(k < chunks)
            def _():
                down_copy(k, i).wait()
                for b in range(nb):
                    ob = jnp.dot(h[b * BR:(b + 1) * BR, :], wbs[i][expert_of(b), 0:ff, :], preferred_element_type=F32)
                    o[b * BR // ALIGN:(b + 1) * BR // ALIGN] = ob.astype(BF16).reshape(BR // ALIGN, ALIGN, CW)

            @pl.when(k + 2 < chunks)
            def _():
                down_copy(k + 2, i).start()

            @pl.when((k >= 1) & (k < chunks + 1))
            def _():
                kk = k - 1
                pair_copy(kk).wait_recv()
                for d in range(n_chip):
                    z[kk, d] = z[kk, d] + drecv[kk, d]
                for cp in s1_copies(kk):
                    cp.start()

            @pl.when(k < chunks)
            def _():
                for d in range(n_chip):
                    dsend[k, d] = combine(0, d)
                pair_copy(k).start()
                for d in range(n_chip):
                    z[k, d] = combine(1, d)

        o[rows // ALIGN:] = jnp.zeros((WIN // ALIGN, ALIGN, CW), BF16)

        @pl.loop(0, (chunks + LAG + 1) // 2)
        def _(k2):
            one_step(k2 * 2, 0)
            one_step(k2 * 2 + 1, 1)

        @pl.loop(0, chunks)
        def _(k):
            pair_copy(k).wait_send()
            for cp in s1_copies(k) + s2_copies(k):
                cp.wait_send()

    pl.run_scoped(give_back, pltpu.VMEM(((rows + WIN) // ALIGN, ALIGN, CW), BF16),
                  pltpu.VMEM((chunks, n_chip, tok, CW), F32), pltpu.VMEM((chunks, n_chip, tok, CW), F32),
                  pltpu.VMEM((chunks, 2, half, CW), F32))


def solution(mesh):
    n_dev = mesh.shape['ep']

    def device_step(tokens, expert_ids, norm_gain, w_router, w_gate, w_up, w_down):
        tok, top_k = expert_ids.shape
        width = tokens.shape[1]
        e_local, _, ff = w_gate.shape
        n_chip = n_dev // 2
        recv_max = 3 * tok * top_k // 2
        nb = (recv_max - e_local) // BR + e_local
        rows = nb * BR
        chunks = width // CW
        dma = pltpu.SemaphoreType.DMA
        half_blk = (chunks, 2, tok // 2, CW)
        tabs = (8 + n_dev * 8, 128)
        wbuf = pltpu.VMEM((e_local, width, 2 * FC), BF16)
        return pl.pallas_call(
            functools.partial(moe_kernel, n_dev, nb, chunks),
            name='moe',
            out_shape=jax.ShapeDtypeStruct((tok, width), BF16),
            in_specs=[VM] * 4 + [ANY] * 3,
            out_specs=VM,
            scratch_shapes=[pltpu.VMEM((n_chip, 2 * tok, width), BF16), wbuf, wbuf,
                            pltpu.VMEM((rows, ff), BF16),
                            pltpu.VMEM((2, n_chip, e_local, tok, WIN), BF16),
                            pltpu.VMEM((2, n_chip, e_local, tok, 128), F32),
                            pltpu.VMEM((n_dev, top_k, tok), I32),
                            pltpu.VMEM((n_dev * 8, tok), F32),
                            pltpu.VMEM(tabs, I32), pltpu.SMEM(tabs, I32),
                            pltpu.VMEM((chunks, n_chip, tok, CW), F32),
                            pltpu.VMEM(half_blk, F32), pltpu.VMEM(half_blk, F32), pltpu.VMEM(half_blk, F32),
                            dma((3, 2)), dma(()), dma((n_dev - 1,)), dma((n_dev,)), dma((14,)), dma((n_dev, 2)),
                            dma((chunks,)), dma((chunks,)),
                            dma((chunks, 4)), dma((chunks, 2)), dma((chunks, 2)), dma((chunks, 2)), dma((chunks, 2))],
            compiler_params=pltpu.CompilerParams(vmem_limit_bytes=67043328, collective_id=0, has_side_effects=True),
        )(tokens, expert_ids.T, norm_gain, w_router.T, w_gate, w_up, w_down)

    row_spec = P(('dp', 'ep'), None)
    expert_spec = P('ep', None, None)
    return jax.shard_map(device_step, mesh=mesh, in_specs=(row_spec, row_spec, P(None), P(None, None), expert_spec, expert_spec, expert_spec), out_specs=row_spec, check_vma=False)
```

time: 402 us -> 104 us (0.26); the launches traced: 398 us -> 104 us
  waiting for transfers between devices: 143 us -> 0 us
  local copies, waits for them, and re-layouts: 106 us -> 1.88 us
  other arithmetic: 45.4 us -> 0 us
  starting transfers between devices: 25.9 us -> 0 us
  Pallas kernels: 77 us -> 102 us
    all_to_all x3 -> x0, waiting for transfers between devices: 143 us -> none  [the longest x1 72.1 us: device_step(): recv_rows = lax.all_to_all(send_rows, 'ep', 0, 0, tiled=True)]
    pallas_call x0 -> x1, Pallas kernels: none -> 102 us  [device_step(): pl.pallas_call(functools.partial(moe_kernel, n_dev, nb, chunks), name='mo...]
    gather x13 -> x0, local copies, waits for them, and re-layouts: 91.7 us -> none  [the longest x1 19.9 us: device_step(): back_rows = expert_out[back_pos].reshape(ep_size, send_max, width)]
    another operation x3 -> x0, Pallas kernels: 75.5 us -> none
    all_to_all x3 -> x0, starting transfers between devices: 25.9 us -> none  [the longest x1 14.9 us: device_step(): home_rows = lax.all_to_all(back_rows, 'ep', 0, 0, tiled=True)]
    convert_element_type x5 -> x0, other arithmetic: 16.9 us -> none  [the longest x1 8.22 us: expert_ffn(): lax.ragged_dot(swiglu_out, w_down, group_sizes, preferred_element_type=jn...]
    scatter x2 -> x0, local copies, waits for them, and re-layouts: 12.6 us -> none  [the longest x1 8.05 us: recv_plan(): jnp.zeros((recv_max,), jnp.int32).at[compact_pos]]
    reduce_sum x6 -> x0, other arithmetic: 8.53 us -> none  [the longest x1 6.52 us: device_step(): moe_sum = jnp.sum(gate_vals[:, :, None] * pair_out, axis=1)]
  transfers between devices with their start and end apart: 3 -> 0, of which waited for: 2 -> 0; matrix products, arithmetic and copies ran while one was open for 18% -> 0% of each run, Pallas kernels for 0% -> 0%
where the time goes in v2:
time: 104 us
  Pallas kernels  102 us (98%)
  local copies, waits for them, and re-layouts  1.88 us (2%)
    pallas_call x1, Pallas kernels, device_step(): pl.pallas_call(functools.partial(moe_kernel, n_dev, nb, chunks), name='mo...  102 us

profile of v2, /device:TPU:81, one launch (start us, length us, event | category | flops | bytes accessed | tf_op | source)
XLA Modules:
  0.0 104.2 jit_solution(9722986114727275714)
XLA Ops:
  0.0 102.3 %moe.1 = bf16[128,2048]{1,0:T(8,128)(2,1)} custom-call(bf16[128,2048]{1,0:T(8,128)(2,1)} %x_ref.1, s32[8,128]{1,0:T(8,128)} %bitcast.3, bf16[2048]{0:T(1024)(128)(2,1)} %g_ref.1, bf16[64,2048]{1,0:T(8,128)(2,1)} %bitcast.2, bf16[8,2048,1024]{2,1,0:T(8,128)(2,1)} %w1_hbm.1, bf16[8,2048,1024]{2,1,0:T(8,128)(2,1)} %w3_hbm.1, bf16[8,1024,2048]{2,1,0:T(8,128)(2,1)} %w2_hbm.1), custom_call_target="tpu_custom_call" | custom-call | tf_op jit(solution)/shard_map/moe/pallas_call | solution.py:362
  102.3 1.9 %copy.9 = bf16[128,2048]{1,0:T(8,128)(2,1)} copy(bf16[128,2048]{1,0:T(8,128)(2,1)} %moe.1) | data formatting | bytes 1048576

commit v3 on v2

--- a/solution.py
+++ b/solution.py
@@ -75,11 +75,11 @@
         for i in range(4):
             x32 = x_ref[i * step:(i + 1) * step, :].astype(F32)
             inv = lax.rsqrt(jnp.mean(x32 * x32, axis=1, keepdims=True) + NORM_EPS)
-            u[chip, pl.ds(pl.multiple_of(core * tok + i * step, step), step), :] = (x32 * inv * gain).astype(BF16)
+            u[chip, pl.ds(pl.multiple_of((i // 2) * tok + core * half + (i % 2) * step, step), step), :] = (x32 * inv * gain).astype(BF16)
         pl.semaphore_wait(barrier, n_dev - 1)
 
         def send(i, blk, hf, peer):
-            ref = u.at[blk // 2, pl.ds(pl.multiple_of((blk % 2) * tok + hf * half, half), half), :]
+            ref = u.at[blk // 2, pl.ds(pl.multiple_of(hf * tok + (blk % 2) * half, half), half), :]
             return rcopy(ref, ref, ssem.at[i], rsem.at[blk, hf], peer)
 
         def ids_send(i, peer):
@@ -147,10 +147,15 @@
         def _(b):
             bf = b.astype(F32)
             mine = (first <= bf) & (bf < last)
-            for s in range(n_dev):
-                sel = jnp.sum(jnp.where(mine, posm[s * 8:(s + 1) * 8, :], 0.0), axis=0, keepdims=True) - (1.0 + BR * bf)
-                p[s // 2, pl.ds(pl.multiple_of(b * BR, BR), BR), (s % 2) * tok:(s % 2 + 1) * tok] = jnp.where(
-                    jnp.broadcast_to(sel, (BR, tok)) == row_i, 1.0, 0.0).astype(BF16)
+            rs = pl.ds(pl.multiple_of(b * BR, BR), BR)
+            sel = [jnp.sum(jnp.where(mine, posm[s * 8:(s + 1) * 8, :], 0.0), axis=0, keepdims=True) - (1.0 + BR * bf)
+                   for s in range(n_dev)]
+            for c in range(n_chip):
+                for hf in range(2):
+                    cut = slice(hf * half, (hf + 1) * half)
+                    both = jnp.concatenate([sel[2 * c][:, cut], sel[2 * c + 1][:, cut]], axis=1)
+                    p[c, rs, hf * tok:(hf + 1) * tok] = jnp.where(
+                        jnp.broadcast_to(both, (BR, tok)) == row_i, 1.0, 0.0).astype(BF16)
 
         def windows():
             wlane = lax.broadcasted_iota(I32, (tok, WIN), 1).astype(F32)
@@ -169,54 +174,59 @@
             mine = pltpu.roll(full, (128 - me * e_local) % 128, 1)
             for k in range(2):
                 par = (k + core + 1) % 2
+                own = jnp.concatenate([mine[k * half:(k + 1) * half], mine[tok + k * half:tok + (k + 1) * half]], axis=0)
                 for e in range(e_local):
-                    gb[par, c, e] = jnp.broadcast_to(mine[k * tok:(k + 1) * tok, e:e + 1], (tok, 128))
+                    gb[par, c, e] = jnp.broadcast_to(own[:, e:e + 1], (tok, 128))
 
         mt, nt = rows // 4, 256
 
-        def gather(cs, first_pass):
+        def gather(pieces, first_pass):
             @pl.loop(0, rows // mt)
             def _(m):
                 rs = pl.ds(pl.multiple_of(m * mt, mt), mt)
+                pick = [p[c, rs, a:b] for c, a, b in pieces]
+                pick = pick[0] if len(pick) == 1 else jnp.concatenate(pick, axis=1)
                 for n in range(width // nt):
                     cols = slice(n * nt, (n + 1) * nt)
-                    part = jnp.dot(p[cs[0], rs, :], u[cs[0], :, cols], preferred_element_type=F32)
-                    for c in cs[1:]:
-                        part = part + jnp.dot(p[c, rs, :], u[c, :, cols], preferred_element_type=F32)
+                    tile = [u[c, a:b, cols] for c, a, b in pieces]
+                    tile = tile[0] if len(tile) == 1 else jnp.concatenate(tile, axis=0)
+                    part = jnp.dot(pick, tile, preferred_element_type=F32).astype(BF16)
                     if first_pass:
-                        xs[rs, cols] = part.astype(BF16)
+                        xs[rs, cols] = part
                     else:
-                        xs[rs, cols] = xs[rs, cols] + part.astype(BF16)
-
+                        xs[rs, cols] = xs[rs, cols] + part
+
+        l_other, r_other, o_own, o_other = lc * 2 + (1 - core), rc * 2 + (1 - core), oc * 2 + core, oc * 2 + (1 - core)
         arrived(partner, 0)
         arrived(partner, 1)
+        gather([(chip, 0, 2 * tok)], True)
         arrived(left, 0)
         forward(6, left, 0, right)
         arrived(right, 1)
         forward(7, right, 1, left)
         forward(8, left, 0, partner)
         forward(9, right, 1, partner)
-        gather([chip], True)
+        windows()
         gates(chip)
+        arrived(l_other, 0)
+        arrived(r_other, 1)
+        gather([(lc, 0, tok), (rc, tok, 2 * tok)], False)
         arrived(left, 1)
         forward(10, left, 1, partner)
         arrived(right, 0)
         forward(11, right, 0, partner)
-        windows()
-        for blk in (lc * 2 + (1 - core), rc * 2 + (1 - core)):
-            arrived(blk, 0)
-            arrived(blk, 1)
-        gather([lc, rc], False)
-        oblk = oc * 2 + core
-        arrived(oblk, 0)
-        forward(12, oblk, 0, partner)
-        arrived(oblk, 1)
-        forward(13, oblk, 1, partner)
+        arrived(l_other, 1)
+        arrived(r_other, 0)
+        gather([(lc, tok, 2 * tok), (rc, 0, tok)], False)
+        arrived(o_own, 0)
+        forward(12, o_own, 0, partner)
+        arrived(o_own, 1)
+        forward(13, o_own, 1, partner)
         gates(lc)
         gates(rc)
-        arrived(oc * 2 + (1 - core), 0)
-        arrived(oc * 2 + (1 - core), 1)
-        gather([oc], False)
+        arrived(o_other, 0)
+        arrived(o_other, 1)
+        gather([(oc, 0, 2 * tok)], False)
         gates(oc)
         tab_copy.wait()
 

time: 104 us -> 103 us (level)
    pallas_call x1, Pallas kernels: 102 us -> 101 us  [device_step(): pl.pallas_call(functools.partial(moe_kernel, n_dev, nb, chunks), name='mo...]
where the time goes in v3:
time: 103 us
  Pallas kernels  101 us (98%)
  local copies, waits for them, and re-layouts  1.88 us (2%)
    pallas_call x1, Pallas kernels, device_step(): pl.pallas_call(functools.partial(moe_kernel, n_dev, nb, chunks), name='mo...  101 us

profile of v3, /device:TPU:81, one launch (start us, length us, event | category | flops | bytes accessed | tf_op | source)
XLA Modules:
  0.0 102.6 jit_solution(15797607393706367981)
XLA Ops:
  0.0 100.7 %moe.1 = bf16[128,2048]{1,0:T(8,128)(2,1)} custom-call(bf16[128,2048]{1,0:T(8,128)(2,1)} %x_ref.1, s32[8,128]{1,0:T(8,128)} %bitcast.3, bf16[2048]{0:T(1024)(128)(2,1)} %g_ref.1, bf16[64,2048]{1,0:T(8,128)(2,1)} %bitcast.2, bf16[8,2048,1024]{2,1,0:T(8,128)(2,1)} %w1_hbm.1, bf16[8,2048,1024]{2,1,0:T(8,128)(2,1)} %w3_hbm.1, bf16[8,1024,2048]{2,1,0:T(8,128)(2,1)} %w2_hbm.1), custom_call_target="tpu_custom_call" | custom-call | tf_op jit(solution)/shard_map/moe/pallas_call | solution.py:372
  100.7 1.9 %copy.9 = bf16[128,2048]{1,0:T(8,128)(2,1)} copy(bf16[128,2048]{1,0:T(8,128)(2,1)} %moe.1) | data formatting | bytes 1048576

commit v4 on v3

--- a/solution.py
+++ b/solution.py
@@ -22,9 +22,9 @@
 VM = pl.BlockSpec(memory_space=pltpu.VMEM)
 
 
-def moe_kernel(n_dev, nb, chunks, x_ref, ids_ref, g_ref, wr_ref, w1_hbm, w3_hbm, w2_hbm, o_ref,
-               u, wb0, wb1, h, pt, gb, ids, posm, tab_v, tab, drecv, r1, rd, r2,
-               wsem, tsem, ids_ssem, ids_rsem, ssem, rsem,
+def moe_kernel(n_dev, nb, chunks, x_hbm, ids_hbm, g_hbm, wr_hbm, w1_hbm, w3_hbm, w2_hbm, o_ref,
+               x_ref, ids_ref, g_ref, wr_ref, u, wb0, wb1, h, pt, gb, ids, posm, tab_v, tab, drecv, r1, rd, r2,
+               insem, wsem, tsem, ids_ssem, ids_rsem, ssem, rsem,
                d_ss, d_rs, s1_ss, r1_rs, rd_rs, s2_ss, r2_rs):
     n_chip = n_dev // 2
     tok, width = x_ref.shape
@@ -62,10 +62,16 @@
     def dispatch(p, xs):
         me, chip, core, rc, lc, oc, right, left, partner = coords()
         others = [(me + i) % n_dev for i in range(1, n_dev)]
+        inputs = [pltpu.make_async_copy(src, dst, insem.at[i]) for i, (src, dst) in enumerate(
+            ((x_hbm, x_ref), (g_hbm, g_ref), (ids_hbm, ids_ref), (wr_hbm, wr_ref)))]
+        for cp in inputs:
+            cp.start()
         barrier = pltpu.get_barrier_semaphore()
         for peer in others:
             pl.semaphore_signal(barrier, inc=1, device_id={'ep': peer}, device_id_type=MESH)
 
+        for cp in inputs:
+            cp.wait()
         for i in range(2):
             for cp in hidden_copies(i, i):
                 cp.start()
@@ -373,9 +379,11 @@
             functools.partial(moe_kernel, n_dev, nb, chunks),
             name='moe',
             out_shape=jax.ShapeDtypeStruct((tok, width), BF16),
-            in_specs=[VM] * 4 + [ANY] * 3,
+            in_specs=[ANY] * 7,
             out_specs=VM,
-            scratch_shapes=[pltpu.VMEM((n_chip, 2 * tok, width), BF16), wbuf, wbuf,
+            scratch_shapes=[pltpu.VMEM((tok, width), BF16), pltpu.VMEM((top_k, tok), I32), pltpu.VMEM((width,), BF16),
+                            pltpu.VMEM((w_router.shape[1], width), BF16),
+                            pltpu.VMEM((n_chip, 2 * tok, width), BF16), wbuf, wbuf,
                             pltpu.VMEM((rows, ff), BF16),
                             pltpu.VMEM((2, n_chip, e_local, tok, WIN), BF16),
                             pltpu.VMEM((2, n_chip, e_local, tok, 128), F32),
@@ -384,7 +392,7 @@
                             pltpu.VMEM(tabs, I32), pltpu.SMEM(tabs, I32),
                             pltpu.VMEM((chunks, n_chip, tok, CW), F32),
                             pltpu.VMEM(half_blk, F32), pltpu.VMEM(half_blk, F32), pltpu.VMEM(half_blk, F32),
-                            dma((3, 2)), dma(()), dma((n_dev - 1,)), dma((n_dev,)), dma((14,)), dma((n_dev, 2)),
+                            dma((4,)), dma((3, 2)), dma(()), dma((n_dev - 1,)), dma((n_dev,)), dma((14,)), dma((n_dev, 2)),
                             dma((chunks,)), dma((chunks,)),
                             dma((chunks, 4)), dma((chunks, 2)), dma((chunks, 2)), dma((chunks, 2)), dma((chunks, 2))],
             compiler_params=pltpu.CompilerParams(vmem_limit_bytes=67043328, collective_id=0, has_side_effects=True),

time: 103 us -> 105 us (1.019)
  Pallas kernels: 101 us -> 103 us
    pallas_call x1, Pallas kernels: 101 us -> 103 us  [device_step(): pl.pallas_call(functools.partial(moe_kernel, n_dev, nb, chunks), name='mo...]
where the time goes in v4:
time: 105 us
  Pallas kernels  103 us (98%)
  local copies, waits for them, and re-layouts  1.88 us (2%)
    pallas_call x1, Pallas kernels, device_step(): pl.pallas_call(functools.partial(moe_kernel, n_dev, nb, chunks), name='mo...  103 us

profile of v4, /device:TPU:81, one launch (start us, length us, event | category | flops | bytes accessed | tf_op | source)
XLA Modules:
  0.0 104.5 jit_solution(16831793346208780331)
XLA Ops:
  0.0 102.7 %moe.1 = bf16[128,2048]{1,0:T(8,128)(2,1)} custom-call(bf16[128,2048]{1,0:T(8,128)(2,1)} %x_hbm.1, s32[8,128]{1,0:T(8,128)} %bitcast.3, bf16[2048]{0:T(1024)(128)(2,1)} %g_hbm.1, bf16[64,2048]{1,0:T(8,128)(2,1)} %bitcast.2, bf16[8,2048,1024]{2,1,0:T(8,128)(2,1)} %w1_hbm.1, bf16[8,2048,1024]{2,1,0:T(8,128)(2,1)} %w3_hbm.1, bf16[8,1024,2048]{2,1,0:T(8,128)(2,1)} %w2_hbm.1), custom_call_target="tpu_custom_call" | custom-call | tf_op jit(solution)/shard_map/moe/pallas_call | solution.py:378
  102.7 1.9 %copy.9 = bf16[128,2048]{1,0:T(8,128)(2,1)} copy(bf16[128,2048]{1,0:T(8,128)(2,1)} %moe.1) | data formatting | bytes 1048576
